TPU v7x, 32 devices: a whole 2x2x4 slice. The times are simulated.
32 devices in a mesh: seq: 16 (over z, y, x), head: 2 (over core).
Axes of the slice: x: 2, y: 2, z: 4, core: 2. Of those that a mesh axis runs over, the one named last changes fastest.
Arguments:
- queries: bfloat16 [8192, 4096], P('seq', 'head'), may hold values from -80 to 80
- new_keys: bfloat16 [8192, 1024], P('seq', 'head'), may hold values from -8 to 8
- new_values: bfloat16 [8192, 1024], P('seq', 'head'), may hold values from -6 to 6
Outputs:
- attended: bfloat16 [8192, 4096], P('seq', 'head')
- key_low: float32 [64, 1024], P('seq', 'head')
- key_step: float32 [64, 1024], P('seq', 'head')
- value_low: float32 [8192], P('seq')
- value_step: float32 [8192], P('seq')
All inputs are finite; a program needn't handle non-finite values.
Results may differ from a plain program's by a relative error of at most 0.0045.
Values may be sent and summed in bfloat16 or wider, within the bound.
A program may use at most 128 MiB of HBM per device.

v0:
```python
import math

import jax
import jax.numpy as jnp
from jax import lax
from jax.sharding import PartitionSpec as P

HEADS = 32
KV_HEADS = 8
HEAD_DIM = 128
WINDOW = 4096
GROUP = 128


negative_fill = -1e30


def passed_along(block, axis, distance):
    devices = range(lax.axis_size(axis))
    route = [(i - distance, i) for i in devices if i - distance in devices]
    return lax.ppermute(block, axis, route)


def shards(queries, new_keys, new_values):
    tok_rows = new_keys.shape[0]
    kv_width = new_keys.shape[1]
    kv_local = kv_width // HEAD_DIM
    group_size = HEADS // KV_HEADS
    halo_count = WINDOW // tok_rows
    scale = 1.0 / math.sqrt(HEAD_DIM)
    stacked = jnp.stack((new_keys, new_values), 0)
    pieces = [stacked]
    latest = stacked
    for distance in range(halo_count):
        latest = passed_along(latest, "seq", 1)
        pieces.insert(0, latest)
    context = jnp.concatenate(pieces, 1)
    total_keys = (halo_count + 1) * tok_rows
    query_size = 512
    key_size = 512
    query_count = tok_rows // query_size
    key_count = total_keys // key_size
    base_pos = lax.axis_index("seq") * tok_rows
    query_heads = queries.reshape(tok_rows, kv_local, group_size, HEAD_DIM)

    def query_step(query_index):
        query_pos = base_pos + query_index * query_size + jnp.arange(query_size, dtype=jnp.int32)

        def key_step(key_index, carry):
            running_max, running_total, running_acc = carry
            key_block = lax.dynamic_slice_in_dim(context, key_index * key_size, key_size, 1)
            key_part = key_block[0].reshape(key_size, kv_local, HEAD_DIM)
            value_part = key_block[1].reshape(key_size, kv_local, HEAD_DIM)
            key_pos = (
                base_pos
                - halo_count * tok_rows
                + key_index * key_size
                + jnp.arange(key_size, dtype=jnp.int32)
            )
            valid = (
                (key_pos[None, :] <= query_pos[:, None])
                & (key_pos[None, :] > query_pos[:, None] - WINDOW)
                & (key_pos[None, :] >= 0)
            )
            scores = (
                jnp.einsum(
                    "qhgd,khd->hgqk", query_heads, key_part, preferred_element_type=jnp.float32
                )
                * scale
            )
            masked = jnp.where(valid[None, None], scores, negative_fill)
            new_max = jnp.maximum(running_max, jnp.max(masked, axis=-1))
            weights = jnp.where(valid[None, None], jnp.exp(masked - new_max[..., None]), 0.0)
            rescale = jnp.exp(running_max - new_max)
            new_total = running_total * rescale + jnp.sum(weights, axis=-1)
            product = jnp.einsum(
                "hgqk,khd->hgqd",
                weights.astype(jnp.bfloat16),
                value_part,
                preferred_element_type=jnp.float32,
            )
            new_acc = running_acc * rescale[..., None] + product
            return (new_max, new_total, new_acc)

        start_max = jnp.full((kv_local, group_size, query_size), negative_fill, jnp.float32)
        start_total = jnp.zeros((kv_local, group_size, query_size), jnp.float32)
        start_acc = jnp.zeros((kv_local, group_size, query_size, HEAD_DIM), jnp.float32)
        final_max, final_total, final_acc = lax.fori_loop(
            0, key_count, key_step, (start_max, start_total, start_acc)
        )
        result = (final_acc / final_total[..., None]).astype(jnp.bfloat16)
        return jnp.transpose(result, (2, 0, 1, 3)).reshape(
            query_size, kv_local * group_size * HEAD_DIM
        )

    attended = lax.map(query_step, jnp.arange(query_count, dtype=jnp.int32)).reshape(
        tok_rows, kv_local * group_size * HEAD_DIM
    )
    grouped = new_keys.astype(jnp.float32).reshape(tok_rows // GROUP, GROUP, kv_width)
    key_low = jnp.min(grouped, axis=1)
    key_step_out = (jnp.max(grouped, axis=1) - key_low) / 3.0
    value_rows = new_values.astype(jnp.float32)
    local_top = jnp.max(value_rows, axis=1)
    local_bottom = jnp.min(value_rows, axis=1)
    row_top = lax.pmax(local_top, "head")
    row_bottom = lax.pmin(local_bottom, "head")
    value_step_out = (row_top - row_bottom) / 3.0
    return (attended, key_low, key_step_out, row_bottom, value_step_out)


def solution(mesh):
    return jax.shard_map(
        shards,
        mesh=mesh,
        in_specs=(P("seq", "head"), P("seq", "head"), P("seq", "head")),
        out_specs=(P("seq", "head"), P("seq", "head"), P("seq", "head"), P("seq"), P("seq")),
        check_vma=False,
    )
```

profile of v0, /device:TPU:14, one launch (start us, length us, event | category | flops | bytes accessed | tf_op | source)
XLA Modules:
  0.0 499.9 jit_solution(18338089420385154287)
XLA Ops:
  7.0 23.4 %collective-permute-done = bf16[2,512,512]{1,2,0:T(8,128)(2,1)S(1)} collective-permute-done((bf16[2,512,512]{1,2,0:T(8,128)(2,1)S(1)}, bf16[2,512,512]{1,2,0:T(8,128)(2,1)S(1)}, u32[]{:S(2)}, u32[]{:S(2)}) %collective-permute-start) | collective-permute-done | bytes 1048608 | tf_op jit(solution)/shard_map/ppermute | solution.py:21
  35.6 21.5 %collective-permute-done.1 = bf16[2,512,512]{1,2,0:T(8,128)(2,1)S(1)} collective-permute-done((bf16[2,512,512]{1,2,0:T(8,128)(2,1)S(1)}, bf16[2,512,512]{1,2,0:T(8,128)(2,1)S(1)}, u32[]{:S(2)}, u32[]{:S(2)}) %collective-permute-start.1) | collective-permute-done | bytes 1048608 | tf_op jit(solution)/shard_map/ppermute | solution.py:21
  64.3 20.7 %collective-permute-done.2 = bf16[2,512,512]{1,2,0:T(8,128)(2,1)S(1)} collective-permute-done((bf16[2,512,512]{1,2,0:T(8,128)(2,1)S(1)}, bf16[2,512,512]{1,2,0:T(8,128)(2,1)S(1)}, u32[]{:S(2)}, u32[]{:S(2)}) %collective-permute-start.2) | collective-permute-done | bytes 1048608 | tf_op jit(solution)/shard_map/ppermute | solution.py:21
  92.2 19.8 %collective-permute-done.3 = bf16[2,512,512]{1,2,0:T(8,128)(2,1)S(1)} collective-permute-done((bf16[2,512,512]{1,2,0:T(8,128)(2,1)S(1)}, bf16[2,512,512]{1,2,0:T(8,128)(2,1)S(1)}, u32[]{:S(2)}, u32[]{:S(2)}) %collective-permute-start.3) | collective-permute-done | bytes 1048608 | tf_op jit(solution)/shard_map/ppermute | solution.py:21
  119.2 19.0 %collective-permute-done.4 = bf16[2,512,512]{1,2,0:T(8,128)(2,1)S(1)} collective-permute-done((bf16[2,512,512]{1,2,0:T(8,128)(2,1)S(1)}, bf16[2,512,512]{1,2,0:T(8,128)(2,1)S(1)}, u32[]{:S(2)}, u32[]{:S(2)}) %collective-permute-start.4) | collective-permute-done | bytes 1048608 | tf_op jit(solution)/shard_map/ppermute | solution.py:21
  145.3 18.1 %collective-permute-done.5 = bf16[2,512,512]{1,2,0:T(8,128)(2,1)S(1)} collective-permute-done((bf16[2,512,512]{1,2,0:T(8,128)(2,1)S(1)}, bf16[2,512,512]{1,2,0:T(8,128)(2,1)S(1)}, u32[]{:S(2)}, u32[]{:S(2)}) %collective-permute-start.5) | collective-permute-done | bytes 1048608 | tf_op jit(solution)/shard_map/ppermute | solution.py:21
  170.6 17.3 %collective-permute-done.6 = bf16[2,512,512]{1,2,0:T(8,128)(2,1)} collective-permute-done((bf16[2,512,512]{1,2,0:T(8,128)(2,1)S(1)}, bf16[2,512,512]{1,2,0:T(8,128)(2,1)}, u32[]{:S(2)}, u32[]{:S(2)}) %collective-permute-start.6) | collective-permute-done | bytes 1048608 | tf_op jit(solution)/shard_map/ppermute | solution.py:21
  225.7 266.9 %while.29 = (s32[]{:T(128)}, f32[4,4,512]{2,1,0:T(4,128)S(1)}, f32[4,4,512]{2,1,0:T(4,128)S(1)}, f32[4,4,512,128]{3,2,1,0:T(8,128)}, s32[]{:T(128)}, /*index=5*/...) while((s32[]{:T(128)}, f32[4,4,512]{2,1,0:T(4,128)S(1)}, ...), condition=%wide.region_3.0_spmd.clone, body=%wide.region_0.3_spmd.clone.sunk | while | flops 2206247424 | bytes 132658424 | solution.py:88
  227.3 9.0 %fusion.32 = (f32[4,4,512]{2,1,0:T(4,128)S(1)}, f32[4,512,512,4]{2,1,3,0:T(8,128)}) fusion(pred[512,512]{0,1:T(8,128)(4,1)S(1)} %and_and_fusion.2, bf16[512,4,128,1]{0,2,3,1:T(8,128)(2,1)S(1)} %bitcast.50, bf16[512,4,4,128]{3,0,2,1:T(8,128)(2,1)} %get-tuple-element.416), kind=kOutput, calls=%fused_computation.3.clone.1 | convolution fusion | flops 1086316544 | bytes 19693568 | tf_op jit(solution)/shard_map/while/body/eval_jaxpr/while/body/eval_jaxpr/qhgd,khd->hgqk/dot_general | solution.py:66
  255.8 9.0 %fusion.32 = (f32[4,4,512]{2,1,0:T(4,128)S(1)}, f32[4,512,512,4]{2,1,3,0:T(8,128)}) fusion(pred[512,512]{0,1:T(8,128)(4,1)S(1)} %and_and_fusion.2, bf16[512,4,128,1]{0,2,3,1:T(8,128)(2,1)S(1)} %bitcast.50, bf16[512,4,4,128]{3,0,2,1:T(8,128)(2,1)} %get-tuple-element.416), kind=kOutput, calls=%fused_computation.3.clone.1 | convolution fusion | flops 1086316544 | bytes 19693568 | tf_op jit(solution)/shard_map/while/body/eval_jaxpr/while/body/eval_jaxpr/qhgd,khd->hgqk/dot_general | solution.py:66
  275.5 8.5 %fusion.35 = f32[4,4,512,128]{3,2,1,0:T(8,128)} fusion(f32[4,4,512,128]{3,2,1,0:T(8,128)} %get-tuple-element.400, f32[4,4,512]{2,1,0:T(4,128)S(1)} %get-tuple-element.382, pred[]{:T(512)S(6)} %compare.3, bf16[512,4,128,1]{0,2,3,1:T(8,128)(2,1)S(1)} %bitcast.51, f32[4,512,512,4]{2,1,3,0:T(8,128)S(1)} %copy-done, ...), kind=kOutput, calls=%fused_computation.9.clone.1 | convolution fusion | flops 1097859072 | bytes 26017792 | tf_op jit(solution)/shard_map/while/body/eval_jaxpr/while/body/eval_jaxpr/hgqk,khd->hgqd/dot_general | solution.py:76
  285.6 9.0 %fusion.32 = (f32[4,4,512]{2,1,0:T(4,128)S(1)}, f32[4,512,512,4]{2,1,3,0:T(8,128)}) fusion(pred[512,512]{0,1:T(8,128)(4,1)S(1)} %and_and_fusion.2, bf16[512,4,128,1]{0,2,3,1:T(8,128)(2,1)S(1)} %bitcast.50, bf16[512,4,4,128]{3,0,2,1:T(8,128)(2,1)} %get-tuple-element.416), kind=kOutput, calls=%fused_computation.3.clone.1 | convolution fusion | flops 1086316544 | bytes 19693568 | tf_op jit(solution)/shard_map/while/body/eval_jaxpr/while/body/eval_jaxpr/qhgd,khd->hgqk/dot_general | solution.py:66
  305.3 8.5 %fusion.35 = f32[4,4,512,128]{3,2,1,0:T(8,128)} fusion(f32[4,4,512,128]{3,2,1,0:T(8,128)} %get-tuple-element.400, f32[4,4,512]{2,1,0:T(4,128)S(1)} %get-tuple-element.382, pred[]{:T(512)S(6)} %compare.3, bf16[512,4,128,1]{0,2,3,1:T(8,128)(2,1)S(1)} %bitcast.51, f32[4,512,512,4]{2,1,3,0:T(8,128)S(1)} %copy-done, ...), kind=kOutput, calls=%fused_computation.9.clone.1 | convolution fusion | flops 1097859072 | bytes 26017792 | tf_op jit(solution)/shard_map/while/body/eval_jaxpr/while/body/eval_jaxpr/hgqk,khd->hgqd/dot_general | solution.py:76
  315.4 9.0 %fusion.32 = (f32[4,4,512]{2,1,0:T(4,128)S(1)}, f32[4,512,512,4]{2,1,3,0:T(8,128)}) fusion(pred[512,512]{0,1:T(8,128)(4,1)S(1)} %and_and_fusion.2, bf16[512,4,128,1]{0,2,3,1:T(8,128)(2,1)S(1)} %bitcast.50, bf16[512,4,4,128]{3,0,2,1:T(8,128)(2,1)} %get-tuple-element.416), kind=kOutput, calls=%fused_computation.3.clone.1 | convolution fusion | flops 1086316544 | bytes 19693568 | tf_op jit(solution)/shard_map/while/body/eval_jaxpr/while/body/eval_jaxpr/qhgd,khd->hgqk/dot_general | solution.py:66
  335.1 8.5 %fusion.35 = f32[4,4,512,128]{3,2,1,0:T(8,128)} fusion(f32[4,4,512,128]{3,2,1,0:T(8,128)} %get-tuple-element.400, f32[4,4,512]{2,1,0:T(4,128)S(1)} %get-tuple-element.382, pred[]{:T(512)S(6)} %compare.3, bf16[512,4,128,1]{0,2,3,1:T(8,128)(2,1)S(1)} %bitcast.51, f32[4,512,512,4]{2,1,3,0:T(8,128)S(1)} %copy-done, ...), kind=kOutput, calls=%fused_computation.9.clone.1 | convolution fusion | flops 1097859072 | bytes 26017792 | tf_op jit(solution)/shard_map/while/body/eval_jaxpr/while/body/eval_jaxpr/hgqk,khd->hgqd/dot_general | solution.py:76
  345.2 9.0 %fusion.32 = (f32[4,4,512]{2,1,0:T(4,128)S(1)}, f32[4,512,512,4]{2,1,3,0:T(8,128)}) fusion(pred[512,512]{0,1:T(8,128)(4,1)S(1)} %and_and_fusion.2, bf16[512,4,128,1]{0,2,3,1:T(8,128)(2,1)S(1)} %bitcast.50, bf16[512,4,4,128]{3,0,2,1:T(8,128)(2,1)} %get-tuple-element.416), kind=kOutput, calls=%fused_computation.3.clone.1 | convolution fusion | flops 1086316544 | bytes 19693568 | tf_op jit(solution)/shard_map/while/body/eval_jaxpr/while/body/eval_jaxpr/qhgd,khd->hgqk/dot_general | solution.py:66
  364.9 8.5 %fusion.35 = f32[4,4,512,128]{3,2,1,0:T(8,128)} fusion(f32[4,4,512,128]{3,2,1,0:T(8,128)} %get-tuple-element.400, f32[4,4,512]{2,1,0:T(4,128)S(1)} %get-tuple-element.382, pred[]{:T(512)S(6)} %compare.3, bf16[512,4,128,1]{0,2,3,1:T(8,128)(2,1)S(1)} %bitcast.51, f32[4,512,512,4]{2,1,3,0:T(8,128)S(1)} %copy-done, ...), kind=kOutput, calls=%fused_computation.9.clone.1 | convolution fusion | flops 1097859072 | bytes 26017792 | tf_op jit(solution)/shard_map/while/body/eval_jaxpr/while/body/eval_jaxpr/hgqk,khd->hgqd/dot_general | solution.py:76
  375.0 9.0 %fusion.32 = (f32[4,4,512]{2,1,0:T(4,128)S(1)}, f32[4,512,512,4]{2,1,3,0:T(8,128)}) fusion(pred[512,512]{0,1:T(8,128)(4,1)S(1)} %and_and_fusion.2, bf16[512,4,128,1]{0,2,3,1:T(8,128)(2,1)S(1)} %bitcast.50, bf16[512,4,4,128]{3,0,2,1:T(8,128)(2,1)} %get-tuple-element.416), kind=kOutput, calls=%fused_computation.3.clone.1 | convolution fusion | flops 1086316544 | bytes 19693568 | tf_op jit(solution)/shard_map/while/body/eval_jaxpr/while/body/eval_jaxpr/qhgd,khd->hgqk/dot_general | solution.py:66
  394.7 8.5 %fusion.35 = f32[4,4,512,128]{3,2,1,0:T(8,128)} fusion(f32[4,4,512,128]{3,2,1,0:T(8,128)} %get-tuple-element.400, f32[4,4,512]{2,1,0:T(4,128)S(1)} %get-tuple-element.382, pred[]{:T(512)S(6)} %compare.3, bf16[512,4,128,1]{0,2,3,1:T(8,128)(2,1)S(1)} %bitcast.51, f32[4,512,512,4]{2,1,3,0:T(8,128)S(1)} %copy-done, ...), kind=kOutput, calls=%fused_computation.9.clone.1 | convolution fusion | flops 1097859072 | bytes 26017792 | tf_op jit(solution)/shard_map/while/body/eval_jaxpr/while/body/eval_jaxpr/hgqk,khd->hgqd/dot_general | solution.py:76
  404.8 9.0 %fusion.32 = (f32[4,4,512]{2,1,0:T(4,128)S(1)}, f32[4,512,512,4]{2,1,3,0:T(8,128)}) fusion(pred[512,512]{0,1:T(8,128)(4,1)S(1)} %and_and_fusion.2, bf16[512,4,128,1]{0,2,3,1:T(8,128)(2,1)S(1)} %bitcast.50, bf16[512,4,4,128]{3,0,2,1:T(8,128)(2,1)} %get-tuple-element.416), kind=kOutput, calls=%fused_computation.3.clone.1 | convolution fusion | flops 1086316544 | bytes 19693568 | tf_op jit(solution)/shard_map/while/body/eval_jaxpr/while/body/eval_jaxpr/qhgd,khd->hgqk/dot_general | solution.py:66
  424.5 8.5 %fusion.35 = f32[4,4,512,128]{3,2,1,0:T(8,128)} fusion(f32[4,4,512,128]{3,2,1,0:T(8,128)} %get-tuple-element.400, f32[4,4,512]{2,1,0:T(4,128)S(1)} %get-tuple-element.382, pred[]{:T(512)S(6)} %compare.3, bf16[512,4,128,1]{0,2,3,1:T(8,128)(2,1)S(1)} %bitcast.51, f32[4,512,512,4]{2,1,3,0:T(8,128)S(1)} %copy-done, ...), kind=kOutput, calls=%fused_computation.9.clone.1 | convolution fusion | flops 1097859072 | bytes 26017792 | tf_op jit(solution)/shard_map/while/body/eval_jaxpr/while/body/eval_jaxpr/hgqk,khd->hgqd/dot_general | solution.py:76
  434.6 9.0 %fusion.32 = (f32[4,4,512]{2,1,0:T(4,128)S(1)}, f32[4,512,512,4]{2,1,3,0:T(8,128)}) fusion(pred[512,512]{0,1:T(8,128)(4,1)S(1)} %and_and_fusion.2, bf16[512,4,128,1]{0,2,3,1:T(8,128)(2,1)S(1)} %bitcast.50, bf16[512,4,4,128]{3,0,2,1:T(8,128)(2,1)} %get-tuple-element.416), kind=kOutput, calls=%fused_computation.3.clone.1 | convolution fusion | flops 1086316544 | bytes 19693568 | tf_op jit(solution)/shard_map/while/body/eval_jaxpr/while/body/eval_jaxpr/qhgd,khd->hgqk/dot_general | solution.py:66
  454.3 8.5 %fusion.35 = f32[4,4,512,128]{3,2,1,0:T(8,128)} fusion(f32[4,4,512,128]{3,2,1,0:T(8,128)} %get-tuple-element.400, f32[4,4,512]{2,1,0:T(4,128)S(1)} %get-tuple-element.382, pred[]{:T(512)S(6)} %compare.3, bf16[512,4,128,1]{0,2,3,1:T(8,128)(2,1)S(1)} %bitcast.51, f32[4,512,512,4]{2,1,3,0:T(8,128)S(1)} %copy-done, ...), kind=kOutput, calls=%fused_computation.9.clone.1 | convolution fusion | flops 1097859072 | bytes 26017792 | tf_op jit(solution)/shard_map/while/body/eval_jaxpr/while/body/eval_jaxpr/hgqk,khd->hgqd/dot_general | solution.py:76
  464.4 9.0 %fusion.32 = (f32[4,4,512]{2,1,0:T(4,128)S(1)}, f32[4,512,512,4]{2,1,3,0:T(8,128)}) fusion(pred[512,512]{0,1:T(8,128)(4,1)S(1)} %and_and_fusion.2, bf16[512,4,128,1]{0,2,3,1:T(8,128)(2,1)S(1)} %bitcast.50, bf16[512,4,4,128]{3,0,2,1:T(8,128)(2,1)} %get-tuple-element.416), kind=kOutput, calls=%fused_computation.3.clone.1 | convolution fusion | flops 1086316544 | bytes 19693568 | tf_op jit(solution)/shard_map/while/body/eval_jaxpr/while/body/eval_jaxpr/qhgd,khd->hgqk/dot_general | solution.py:66
  (174 shorter events, 218.4 us)
Async XLA Ops:
  0.6 204.2 %copy-start.2 = (bf16[512,512]{1,0:T(8,128)(2,1)S(1)}, bf16[512,512]{1,0:T(8,128)(2,1)}, u32[]{:S(2)}) copy-start(bf16[512,512]{1,0:T(8,128)(2,1)} %param.6) | copy-start | bytes 1572868
  0.6 198.8 %copy-start.1 = (bf16[512,512]{1,0:T(8,128)(2,1)S(1)}, bf16[512,512]{1,0:T(8,128)(2,1)}, u32[]{:S(2)}) copy-start(bf16[512,512]{1,0:T(8,128)(2,1)} %param.7) | copy-start | bytes 1572868
  2.0 192.2 %copy-start.3 = (bf16[512,512]{0,1:T(8,128)(2,1)}, bf16[512,512]{0,1:T(8,128)(2,1)S(1)}, u32[]{:S(2)}) copy-start(bf16[512,512]{0,1:T(8,128)(2,1)S(1)} %copy.13) | copy-start | bytes 1572868
  3.5 190.7 %copy-start.5 = (bf16[512,512]{0,1:T(8,128)(2,1)}, bf16[512,512]{0,1:T(8,128)(2,1)S(1)}, u32[]{:S(2)}) copy-start(bf16[512,512]{0,1:T(8,128)(2,1)S(1)} %copy.14) | copy-start | bytes 1572868
  3.6 26.8 %collective-permute-start = (bf16[2,512,512]{1,2,0:T(8,128)(2,1)S(1)}, bf16[2,512,512]{1,2,0:T(8,128)(2,1)S(1)}, u32[]{:S(2)}, u32[]{:S(2)}) collective-permute-start(bf16[2,512,512]{1,2,0:T(8,128)(2,1)S(1)} %pad_maximum_fusion), channel_id=1, source_target_pairs={{0,2},{2,4},{4,6},{6,8},{8,10},{10,12},{12,14},{14,16},{16,18},{18... | collective-permute-start | bytes 3145736 | tf_op jit(solution)/shard_map/ppermute | solution.py:21
  30.4 163.8 %copy-start.7 = (bf16[2,512,512]{1,2,0:T(8,128)(2,1)}, bf16[2,512,512]{1,2,0:T(8,128)(2,1)S(1)}, u32[]{:S(2)}) copy-start(bf16[2,512,512]{1,2,0:T(8,128)(2,1)S(1)} %collective-permute-done) | copy-start | bytes 3145732
  30.4 26.7 %collective-permute-start.1 = (bf16[2,512,512]{1,2,0:T(8,128)(2,1)S(1)}, bf16[2,512,512]{1,2,0:T(8,128)(2,1)S(1)}, u32[]{:S(2)}, u32[]{:S(2)}) collective-permute-start(bf16[2,512,512]{1,2,0:T(8,128)(2,1)S(1)} %collective-permute-done), channel_id=1, source_target_pairs={{0,2},{2,4},{4,6},{6,8},{8,10},{10,12},{12,14},{14,16},{16,18},{18... | collective-permute-start | bytes 3145736 | tf_op jit(solution)/shard_map/ppermute | solution.py:21
  58.1 26.9 %collective-permute-start.2 = (bf16[2,512,512]{1,2,0:T(8,128)(2,1)S(1)}, bf16[2,512,512]{1,2,0:T(8,128)(2,1)S(1)}, u32[]{:S(2)}, u32[]{:S(2)}) collective-permute-start(bf16[2,512,512]{1,2,0:T(8,128)(2,1)S(1)} %collective-permute-done.1), channel_id=1, source_target_pairs={{0,2},{2,4},{4,6},{6,8},{8,10},{10,12},{12,14},{14,16},{16,18},{18... | collective-permute-start | bytes 3145736 | tf_op jit(solution)/shard_map/ppermute | solution.py:21
  86.0 26.0 %collective-permute-start.3 = (bf16[2,512,512]{1,2,0:T(8,128)(2,1)S(1)}, bf16[2,512,512]{1,2,0:T(8,128)(2,1)S(1)}, u32[]{:S(2)}, u32[]{:S(2)}) collective-permute-start(bf16[2,512,512]{1,2,0:T(8,128)(2,1)S(1)} %collective-permute-done.2), channel_id=1, source_target_pairs={{0,2},{2,4},{4,6},{6,8},{8,10},{10,12},{12,14},{14,16},{16,18},{18... | collective-permute-start | bytes 3145736 | tf_op jit(solution)/shard_map/ppermute | solution.py:21
  113.0 25.2 %collective-permute-start.4 = (bf16[2,512,512]{1,2,0:T(8,128)(2,1)S(1)}, bf16[2,512,512]{1,2,0:T(8,128)(2,1)S(1)}, u32[]{:S(2)}, u32[]{:S(2)}) collective-permute-start(bf16[2,512,512]{1,2,0:T(8,128)(2,1)S(1)} %collective-permute-done.3), channel_id=1, source_target_pairs={{0,2},{2,4},{4,6},{6,8},{8,10},{10,12},{12,14},{14,16},{16,18},{18... | collective-permute-start | bytes 3145736 | tf_op jit(solution)/shard_map/ppermute | solution.py:21
  139.1 24.3 %collective-permute-start.5 = (bf16[2,512,512]{1,2,0:T(8,128)(2,1)S(1)}, bf16[2,512,512]{1,2,0:T(8,128)(2,1)S(1)}, u32[]{:S(2)}, u32[]{:S(2)}) collective-permute-start(bf16[2,512,512]{1,2,0:T(8,128)(2,1)S(1)} %collective-permute-done.4), channel_id=1, source_target_pairs={{0,2},{2,4},{4,6},{6,8},{8,10},{10,12},{12,14},{14,16},{16,18},{18... | collective-permute-start | bytes 3145736 | tf_op jit(solution)/shard_map/ppermute | solution.py:21
  164.4 23.4 %collective-permute-start.6 = (bf16[2,512,512]{1,2,0:T(8,128)(2,1)S(1)}, bf16[2,512,512]{1,2,0:T(8,128)(2,1)}, u32[]{:S(2)}, u32[]{:S(2)}) collective-permute-start(bf16[2,512,512]{1,2,0:T(8,128)(2,1)S(1)} %collective-permute-done.5), channel_id=1, source_target_pairs={{0,2},{2,4},{4,6},{6,8},{8,10},{10,12},{12,14},{14,16},{16,18},{18... | collective-permute-start | bytes 3145736 | tf_op jit(solution)/shard_map/ppermute | solution.py:21
  187.8 23.0 %collective-permute-start.7 = (bf16[2,512,512]{1,2,0:T(8,128)(2,1)}, bf16[2,512,512]{1,2,0:T(8,128)(2,1)}, u32[]{:S(2)}, u32[]{:S(2)}) collective-permute-start(bf16[2,512,512]{1,2,0:T(8,128)(2,1)} %collective-permute-done.6), channel_id=1, source_target_pairs={{0,2},{2,4},{4,6},{6,8},{8,10},{10,12},{12,14},{14,16},{16,18},{18... | collective-permute-start | bytes 3145736 | tf_op jit(solution)/shard_map/ppermute | solution.py:21
  199.4 24.0 %copy-start.8 = (bf16[2,512,512]{1,2,0:T(8,128)(2,1)S(1)}, bf16[2,512,512]{1,2,0:T(8,128)(2,1)}, u32[]{:S(2)}) copy-start(bf16[2,512,512]{1,2,0:T(8,128)(2,1)} %copy-done.7) | copy-start | bytes 3145732
  199.4 25.1 %copy-start.4 = (bf16[512,512]{0,1:T(8,128)(2,1)S(1)}, bf16[512,512]{0,1:T(8,128)(2,1)}, u32[]{:S(2)}) copy-start(bf16[512,512]{0,1:T(8,128)(2,1)} %copy-done.3) | copy-start | bytes 1572868
  199.4 25.1 %copy-start.6 = (bf16[512,512]{0,1:T(8,128)(2,1)S(1)}, bf16[512,512]{0,1:T(8,128)(2,1)}, u32[]{:S(2)}) copy-start(bf16[512,512]{0,1:T(8,128)(2,1)} %copy-done.5) | copy-start | bytes 1572868
  204.8 20.9 %copy-start.18 = (f32[512]{0:T(512)}, f32[512]{0:T(512)S(1)}, u32[]{:S(2)}) copy-start(f32[512]{0:T(512)S(1)} %pmin.7) | copy-start | bytes 6148
  204.8 15.3 %copy-start.14 = (bf16[2,512,512]{1,2,0:T(8,128)(2,1)S(1)}, bf16[2,512,512]{1,2,0:T(8,128)(2,1)}, u32[]{:S(2)}) copy-start(bf16[2,512,512]{1,2,0:T(8,128)(2,1)} %copy-done.13) | copy-start | bytes 3145732
  204.8 16.4 %copy-start.12 = (bf16[2,512,512]{1,2,0:T(8,128)(2,1)S(1)}, bf16[2,512,512]{1,2,0:T(8,128)(2,1)}, u32[]{:S(2)}) copy-start(bf16[2,512,512]{1,2,0:T(8,128)(2,1)} %copy-done.11) | copy-start | bytes 3145732
  204.8 17.6 %copy-start.10 = (bf16[2,512,512]{1,2,0:T(8,128)(2,1)S(1)}, bf16[2,512,512]{1,2,0:T(8,128)(2,1)}, u32[]{:S(2)}) copy-start(bf16[2,512,512]{1,2,0:T(8,128)(2,1)} %copy-done.9) | copy-start | bytes 3145732
  204.9 20.7 %copy-start.17 = (f32[4,512]{1,0:T(4,128)}, f32[4,512]{1,0:T(4,128)S(1)}, u32[]{:S(2)}) copy-start(f32[4,512]{1,0:T(4,128)S(1)} %convert_reduce_fusion.1) | copy-start | bytes 24580
  264.8 10.7 %copy-start = (f32[4,512,512,4]{2,1,3,0:T(8,128)S(1)}, f32[4,512,512,4]{2,1,3,0:T(8,128)}, u32[]{:S(2)}) copy-start(f32[4,512,512,4]{2,1,3,0:T(8,128)} %get-tuple-element.380) | copy-start | bytes 50331652 | tf_op jit(solution)/shard_map/while/body/eval_jaxpr/while
  354.2 10.7 %copy-start = (f32[4,512,512,4]{2,1,3,0:T(8,128)S(1)}, f32[4,512,512,4]{2,1,3,0:T(8,128)}, u32[]{:S(2)}) copy-start(f32[4,512,512,4]{2,1,3,0:T(8,128)} %get-tuple-element.380) | copy-start | bytes 50331652 | tf_op jit(solution)/shard_map/while/body/eval_jaxpr/while
  384.0 10.7 %copy-start = (f32[4,512,512,4]{2,1,3,0:T(8,128)S(1)}, f32[4,512,512,4]{2,1,3,0:T(8,128)}, u32[]{:S(2)}) copy-start(f32[4,512,512,4]{2,1,3,0:T(8,128)} %get-tuple-element.380) | copy-start | bytes 50331652 | tf_op jit(solution)/shard_map/while/body/eval_jaxpr/while
  (11 other events, 69.0 us)
where the time goes:
time: 505 us; the launch traced here: 500 us
  matrix products  156 us (31%)
  waiting for transfers between devices  144 us (29%)
  other arithmetic  82.6 us (16%)
  local copies, waits for them, and re-layouts  64.7 us (13%)
  starting transfers between devices  45.7 us (9%)
  blocking collectives  5.07 us (1%)
    ppermute x8, waiting for transfers between devices, passed_along(): return lax.ppermute(block, axis, route)  144 us
    dot_general x9, matrix products, key_step(): jnp.einsum('qhgd,khd->hgqk', query_heads, key_part, preferred_element_typ...  80.9 us
    dot_general x9, matrix products, key_step(): jnp.einsum('hgqk,khd->hgqd', weights.astype(jnp.bfloat16), value_part, pr...  75.2 us
    reduce_sum x9, other arithmetic, key_step(): new_total = running_total * rescale + jnp.sum(weights, axis=-1)  73.3 us
    ppermute x8, starting transfers between devices, passed_along(): return lax.ppermute(block, axis, route)  45.7 us
    unnamed x48, local copies, waits for them, and re-layouts  26.7 us
    while x27, local copies, waits for them, and re-layouts  22.1 us
    slice x9, local copies, waits for them, and re-layouts, key_step(): value_part = key_block[1].reshape(key_size, kv_local, HEAD_DIM)  11.5 us
  transfers between devices with their start and end apart: 8, of which 8 were waited for; matrix products, arithmetic and copies ran while one was open for 1% of the time, Pallas kernels for 0%

commit v1 on v0

v1 whole, which is shorter than its diff:
```python
import functools
import math

import jax
import jax.numpy as jnp
from jax import lax
from jax.experimental import pallas as pl
from jax.experimental.pallas import tpu as pltpu
from jax.sharding import PartitionSpec as P

HEADS = 32
KV_HEADS = 8
HEAD_DIM = 128
WINDOW = 4096
GROUP = 128

negative_fill = -1e30
query_tile = 256

OWN, FAR, NEAR, NEAR_A, NEAR_B, NEAR_C, MIX_A, MIX_B, MIX_C = range(9)


def attend_kernel(
    devices, layer, q_hbm, k_hbm, v_hbm, o_hbm, q_buf, o_buf, kv, acc, peak,
    q_sem, in_sem, out_sem, send_sem, recv_sem,
):
    rows = q_buf.shape[1]
    local = kv.shape[1]
    group = q_buf.shape[0] // local
    factor = math.log2(math.e) / math.sqrt(HEAD_DIM)
    me = lax.axis_index("seq")
    plane = me // layer
    place = lax.rem(me, layer)
    up = lax.rem(me + layer, devices)
    down = lax.rem(me + devices - layer, devices)
    bit_a = lax.rem(place, 2)
    bit_b = place // 2
    side_a = me + 1 - 2 * bit_a
    side_b = me + 2 - 4 * bit_b

    def q_copy(head, sub):
        col = pl.multiple_of((head * group + sub) * HEAD_DIM, HEAD_DIM)
        return pltpu.make_async_copy(
            q_hbm.at[:, pl.ds(col, HEAD_DIM)], q_buf.at[head * group + sub], q_sem.at[head, sub]
        )

    def out_copy(head, sub):
        col = pl.multiple_of((head * group + sub) * HEAD_DIM, HEAD_DIM)
        return pltpu.make_async_copy(
            o_buf.at[head * group + sub], o_hbm.at[:, pl.ds(col, HEAD_DIM)], out_sem.at[head, sub]
        )

    def own_copy(head, which):
        col = pl.multiple_of(head * HEAD_DIM, HEAD_DIM)
        source = (k_hbm, v_hbm)[which]
        return pltpu.make_async_copy(
            source.at[:, pl.ds(col, HEAD_DIM)], kv.at[OWN, head, which], in_sem.at[head, which]
        )

    def send(head, source, slot, target):
        return pltpu.make_async_remote_copy(
            src_ref=kv.at[source, head],
            dst_ref=kv.at[slot, head],
            send_sem=send_sem.at[slot, head],
            recv_sem=recv_sem.at[slot, head],
            device_id={"seq": target},
            device_id_type=pl.DeviceIdType.MESH,
        )

    routes = {
        NEAR: (OWN, up),
        FAR: (NEAR, up),
        NEAR_A: (NEAR, side_a),
        NEAR_B: (NEAR, side_b),
        NEAR_C: (NEAR_A, side_b),
        MIX_A: (bit_a, side_a),
        MIX_B: (bit_b, side_b),
        MIX_C: (MIX_B, side_a),
    }

    def transfer(head, slot):
        source, target = routes[slot]
        return send(head, source, slot, target)

    barrier = pltpu.get_barrier_semaphore()
    for other in (up, down, side_a, side_b):
        pl.semaphore_signal(
            barrier, inc=1, device_id={"seq": other}, device_id_type=pl.DeviceIdType.MESH
        )
    for head in range(local):
        for which in range(2):
            own_copy(head, which).start()
    for head in range(local):
        for sub in range(group):
            q_copy(head, sub).start()
    pl.semaphore_wait(barrier, 4)

    tiles = rows // query_tile

    def scores_of(q, slot, head):
        return lax.dot_general(
            q, kv[slot, head, 0], (((1,), (1,)), ((), ())), preferred_element_type=jnp.float32
        )

    def product_of(weights, slot, head):
        values = kv[slot, head, 1]
        wide = jnp.concatenate((values, jnp.ones_like(values)), 1)
        return jnp.dot(weights.astype(jnp.bfloat16), wide, preferred_element_type=jnp.float32)

    def step(head, slots, first=False):
        @pl.loop(0, group * tiles)
        def _(index):
            sub = index // tiles
            start = pl.multiple_of(lax.rem(index, tiles) * query_tile, query_tile)
            state = pl.ds(pl.multiple_of(index * query_tile, query_tile), query_tile)
            q = q_buf[head * group + sub, pl.ds(start, query_tile), :]
            scores = []
            for slot in slots:
                part = scores_of(q, slot, head)
                if slot == OWN:
                    row = start + lax.broadcasted_iota(jnp.int32, part.shape, 0)
                    column = lax.broadcasted_iota(jnp.int32, part.shape, 1)
                    near = column <= row
                    far = scores_of(q, FAR, head)
                    far = jnp.where(plane >= 2, far, negative_fill)
                    part = jnp.where(near, part, far)
                scores.append(part)
            top = functools.reduce(jnp.maximum, scores)
            top = jnp.max(top, axis=1, keepdims=True)
            if not first:
                before = peak[state, :]
                top = jnp.maximum(before, top)
                fade = jnp.exp2((before - top) * factor)
                peak[state, :] = top
            else:
                peak[state, :] = jnp.broadcast_to(top, (query_tile, HEAD_DIM))
            top = top[:, :1]
            total = None
            for slot, part in zip(slots, scores):
                weights = jnp.exp2((part - top) * factor)
                if slot == OWN:
                    product = product_of(jnp.where(near, weights, 0.0), OWN, head)
                    product += product_of(jnp.where(near, 0.0, weights), FAR, head)
                else:
                    product = product_of(weights, slot, head)
                total = product if total is None else total + product
            if first:
                acc[state, :] = total
            else:
                acc[state, :HEAD_DIM] = acc[state, :HEAD_DIM] * fade + total[:, :HEAD_DIM]
                acc[state, HEAD_DIM:] = acc[state, HEAD_DIM:] * fade + total[:, HEAD_DIM:]

    def steps(head, valid, all_valid, slots, first=False):
        @pl.when(all_valid)
        def _():
            step(head, slots, first)

        @pl.when(jnp.logical_not(all_valid))
        def _():
            for at, (slot, good) in enumerate(zip(slots, valid)):
                if good is None:
                    step(head, (slot,), first and at == 0)
                else:
                    pl.when(good)(functools.partial(step, head, (slot,)))

    def finish(head):
        for sub in range(group):
            spot = pl.ds(sub * rows, rows)
            o_buf[head * group + sub] = (
                acc[spot, :HEAD_DIM] / acc[spot, HEAD_DIM:]
            ).astype(o_buf.dtype)
            out_copy(head, sub).start()

    near_ok = plane >= 1
    far_ok = plane >= 2
    mix_a_ok = (plane >= 2) | (bit_a == 1)
    mix_b_ok = (plane >= 2) | (bit_b == 1)

    @pl.loop(0, local + 1)
    def _(now):
        last = now - 1

        @pl.when(now < local)
        def _():
            for which in range(2):
                own_copy(now, which).wait()
            transfer(now, NEAR).start()

        @pl.when(now >= 1)
        def _():
            transfer(last, MIX_B).wait_recv()
            transfer(last, MIX_A).wait_recv()
            transfer(last, MIX_C).start()
            transfer(last, NEAR_C).start()
            steps(last, (near_ok, mix_a_ok, mix_b_ok), far_ok, (NEAR_B, MIX_A, MIX_B))

        @pl.when(now < local)
        def _():
            transfer(now, NEAR).wait_recv()
            transfer(now, NEAR_A).start()
            transfer(now, NEAR_B).start()
            transfer(now, FAR).start()

        @pl.when(now >= 1)
        def _():
            transfer(last, MIX_C).wait_recv()
            transfer(last, NEAR_C).wait_recv()
            steps(last, (near_ok, mix_b_ok), far_ok, (NEAR_C, MIX_C))
            finish(last)

        @pl.when(now < local)
        def _():
            transfer(now, FAR).wait_recv()
            transfer(now, MIX_A).start()
            transfer(now, MIX_B).start()
            transfer(now, NEAR_A).wait_recv()
            transfer(now, NEAR_B).wait_recv()
            for sub in range(group):
                q_copy(now, sub).wait()
            steps(now, (None, near_ok, near_ok), near_ok, (OWN, NEAR, NEAR_A), True)

    @pl.loop(0, local)
    def _(head):
        for slot in routes:
            transfer(head, slot).wait_send()
        for sub in range(group):
            out_copy(head, sub).wait()


def attend(devices, queries, new_keys, new_values):
    rows, width = queries.shape
    local = new_keys.shape[1] // HEAD_DIM
    heads = width // HEAD_DIM
    group = heads // local
    halo = WINDOW // rows
    layer = halo // 2
    if layer != 4 or devices % layer or devices < 3 * layer:
        raise ValueError("window layout")
    kernel = functools.partial(attend_kernel, devices, layer)
    hbm = pl.BlockSpec(memory_space=pl.ANY)
    return pl.pallas_call(
        kernel,
        out_shape=jax.ShapeDtypeStruct(queries.shape, jnp.bfloat16),
        in_specs=[hbm] * 3,
        out_specs=hbm,
        scratch_shapes=[
            pltpu.VMEM((heads, rows, HEAD_DIM), jnp.bfloat16),
            pltpu.VMEM((heads, rows, HEAD_DIM), jnp.bfloat16),
            pltpu.VMEM((9, local, 2, rows, HEAD_DIM), jnp.bfloat16),
            pltpu.VMEM((group * rows, 2 * HEAD_DIM), jnp.float32),
            pltpu.VMEM((group * rows, HEAD_DIM), jnp.float32),
            pltpu.SemaphoreType.DMA((local, group)),
            pltpu.SemaphoreType.DMA((local, 2)),
            pltpu.SemaphoreType.DMA((local, group)),
            pltpu.SemaphoreType.DMA((9, local)),
            pltpu.SemaphoreType.DMA((9, local)),
        ],
        compiler_params=pltpu.CompilerParams(
            collective_id=0, has_side_effects=True, vmem_limit_bytes=60 * 1024 * 1024
        ),
        cost_estimate=pl.CostEstimate(
            flops=4 * rows * width * WINDOW,
            bytes_accessed=2 * 2 * rows * width,
            transcendentals=heads * rows * WINDOW,
        ),
    )(queries, new_keys, new_values)


def over_heads(values, devices, combine):
    distance = 1
    while distance < devices:
        route = [(i, i ^ distance) for i in range(devices)]
        values = combine(values, lax.ppermute(values, "head", route))
        distance *= 2
    return values


def shards(mesh_shape, queries, new_keys, new_values):
    tok_rows, kv_width = new_keys.shape
    value_rows = new_values.astype(jnp.float32)
    extremes = jnp.stack((jnp.max(value_rows, axis=1), -jnp.min(value_rows, axis=1)), 0)
    extremes = over_heads(extremes, mesh_shape["head"], jnp.maximum)
    row_bottom = -extremes[1]
    value_step_out = (extremes[0] - row_bottom) / 3.0
    grouped = new_keys.astype(jnp.float32).reshape(tok_rows // GROUP, GROUP, kv_width)
    key_low = jnp.min(grouped, axis=1)
    key_step_out = (jnp.max(grouped, axis=1) - key_low) / 3.0
    attended = attend(mesh_shape["seq"], queries, new_keys, new_values)
    return (attended, key_low, key_step_out, row_bottom, value_step_out)


def solution(mesh):
    return jax.shard_map(
        functools.partial(shards, dict(mesh.shape)),
        mesh=mesh,
        in_specs=(P("seq", "head"), P("seq", "head"), P("seq", "head")),
        out_specs=(P("seq", "head"), P("seq", "head"), P("seq", "head"), P("seq"), P("seq")),
        check_vma=False,
    )
```

time: 505 us -> 188 us (0.37)
  Pallas kernels: 0 us -> 178 us
  matrix products: 156 us -> 0 us
  waiting for transfers between devices: 144 us -> 0.01 us
  other arithmetic: 82.6 us -> 5.88 us
  local copies, waits for them, and re-layouts: 64.7 us -> 3.17 us
  starting transfers between devices: 45.7 us -> 0.07 us
  blocking collectives: 5.07 us -> 0 us
    pallas_call x0 -> x1, Pallas kernels: none -> 178 us  [attend(): pl.pallas_call(kernel, out_shape=jax.ShapeDtypeStruct(queries.shape, jnp....]
    dot_general x18 -> x0, matrix products: 156 us -> none  [the longest x9 80.9 us: key_step(): jnp.einsum('qhgd,khd->hgqk', query_heads, key_part, preferred_element_typ...]
    ppermute x8 -> x1, waiting for transfers between devices: 144 us -> 0.01 us  [over_heads(): values = combine(values, lax.ppermute(values, 'head', route))]
    reduce_sum x9 -> x0, other arithmetic: 73.3 us -> none  [key_step(): new_total = running_total * rescale + jnp.sum(weights, axis=-1)]
    ppermute x8 -> x1, starting transfers between devices: 45.7 us -> 0.07 us  [over_heads(): values = combine(values, lax.ppermute(values, 'head', route))]
    unnamed x48 -> x5, local copies, waits for them, and re-layouts: 26.7 us -> 3.17 us
    while x27 -> x0, local copies, waits for them, and re-layouts: 22.1 us -> none
    slice x9 -> x0, local copies, waits for them, and re-layouts: 11.5 us -> none  [key_step(): value_part = key_block[1].reshape(key_size, kv_local, HEAD_DIM)]
  transfers between devices with their start and end apart: 8 -> 1, of which waited for: 8 -> 0; matrix products, arithmetic and copies ran while one was open for 1% -> 2% of each run, Pallas kernels for 0% -> 95%
where the time goes in v1:
time: 188 us
  Pallas kernels  178 us (95%)
  other arithmetic  5.88 us (3%)
  local copies, waits for them, and re-layouts  3.17 us (2%)
    pallas_call x1, Pallas kernels, attend(): pl.pallas_call(kernel, out_shape=jax.ShapeDtypeStruct(queries.shape, jnp....  178 us
  transfers between devices with their start and end apart: 1, of which 0 were waited for; matrix products, arithmetic and copies ran while one was open for 2% of the time, Pallas kernels for 95%

profile of v1, /device:TPU:14, one launch (start us, length us, event | category | flops | bytes accessed | tf_op | source)
XLA Modules:
  0.0 187.8 jit_solution(7919395995854178215)
XLA Ops:
  0.6 1.2 convert_reduce_fusion
  1.8 1.2 reduce_max.26
  3.1 0.1 collective-permute-start
  3.1 1.1 convert_reduce_fusion.1
  4.3 0.0 copy-start
  4.3 1.1 bitcast_reduce_fusion
  5.4 178.0 %shard_map.74 = bf16[512,2048]{1,0:T(8,128)(2,1)} custom-call(bf16[512,2048]{1,0:T(8,128)(2,1)} %q_hbm.1, bf16[512,512]{1,0:T(8,128)(2,1)} %k_hbm.1, bf16[512,512]{1,0:T(8,128)(2,1)} %v_hbm.1), custom_call_target="tpu_custom_call" | custom-call | flops 17179869184 | bytes 4194304 | tf_op jit(solution)/shard_map/pallas_call | solution.py:241
  183.4 0.0 copy-done
  183.4 0.6 fusion
  184.0 0.0 collective-permute-done
  184.0 0.0 copy-start.1
  184.0 0.6 subtract_multiply_fusion
  184.6 3.2 %copy.9 = bf16[512,2048]{1,0:T(8,128)(2,1)} copy(bf16[512,2048]{1,0:T(8,128)(2,1)} %shard_map.74) | data formatting | bytes 4194304
  187.8 0.0 copy-done.1
  (5 shorter events, 0.0 us)
Async XLA Ops:
  3.1 180.9 %collective-permute-start = (f32[2,512]{1,0:T(2,128)S(1)}, f32[2,512]{1,0:T(2,128)S(1)}, u32[]{:S(2)}, u32[]{:S(2)}) collective-permute-start(f32[2,512]{1,0:T(2,128)S(1)} %pad_maximum_fusion), channel_id=1, source_target_pairs={{0,1},{1,0},{2,3},{3,2},{4,5},{5,4},{6,7},{7,6},{8,9},{9,8},{10,11... | collective-permute-start | bytes 12296 | tf_op jit(solution)/shard_map/ppermute | solution.py:273
  4.3 179.1 %copy-start = (f32[4,512]{1,0:T(4,128)}, f32[4,512]{1,0:T(4,128)S(1)}, u32[]{:S(2)}) copy-start(f32[4,512]{1,0:T(4,128)S(1)} %convert_reduce_fusion.1) | copy-start | bytes 24580
  184.0 3.8 %copy-start.1 = (f32[1,512]{1,0:T(1,128)}, f32[1,512]{1,0:T(1,128)S(1)}, u32[]{:S(2)}) copy-start(f32[1,512]{1,0:T(1,128)S(1)} %get-tuple-element.6) | copy-start | bytes 6148

commit v2 on v1

--- a/solution.py
+++ b/solution.py
@@ -15,7 +15,7 @@
 GROUP = 128
 
 negative_fill = -1e30
-query_tile = 256
+query_heads = 2
 
 OWN, FAR, NEAR, NEAR_A, NEAR_B, NEAR_C, MIX_A, MIX_B, MIX_C = range(9)
 
@@ -24,9 +24,10 @@
     devices, layer, q_hbm, k_hbm, v_hbm, o_hbm, q_buf, o_buf, kv, acc, peak,
     q_sem, in_sem, out_sem, send_sem, recv_sem,
 ):
-    rows = q_buf.shape[1]
+    rows = o_buf.shape[1]
     local = kv.shape[1]
-    group = q_buf.shape[0] // local
+    group = o_buf.shape[0] // local
+    query_tile = query_heads * rows
     factor = math.log2(math.e) / math.sqrt(HEAD_DIM)
     me = lax.axis_index("seq")
     plane = me // layer
@@ -41,7 +42,7 @@
     def q_copy(head, sub):
         col = pl.multiple_of((head * group + sub) * HEAD_DIM, HEAD_DIM)
         return pltpu.make_async_copy(
-            q_hbm.at[:, pl.ds(col, HEAD_DIM)], q_buf.at[head * group + sub], q_sem.at[head, sub]
+            q_hbm.at[:, pl.ds(col, HEAD_DIM)], q_buf.at[head, pl.ds(sub * rows, rows)], q_sem.at[head, sub]
         )
 
     def out_copy(head, sub):
@@ -82,6 +83,11 @@
         source, target = routes[slot]
         return send(head, source, slot, target)
 
+    near_ok = plane >= 1
+    far_ok = plane >= 2
+    mix_a_ok = (plane >= 2) | (bit_a == 1)
+    mix_b_ok = (plane >= 2) | (bit_b == 1)
+
     barrier = pltpu.get_barrier_semaphore()
     for other in (up, down, side_a, side_b):
         pl.semaphore_signal(
@@ -95,7 +101,8 @@
             q_copy(head, sub).start()
     pl.semaphore_wait(barrier, 4)
 
-    tiles = rows // query_tile
+    def lane_parts(block):
+        return [block[:, at : at + HEAD_DIM] for at in range(0, block.shape[1], HEAD_DIM)]
 
     def scores_of(q, slot, head):
         return lax.dot_general(
@@ -103,29 +110,33 @@
         )
 
     def product_of(weights, slot, head):
-        values = kv[slot, head, 1]
-        wide = jnp.concatenate((values, jnp.ones_like(values)), 1)
-        return jnp.dot(weights.astype(jnp.bfloat16), wide, preferred_element_type=jnp.float32)
-
-    def step(head, slots, first=False):
-        @pl.loop(0, group * tiles)
+        product = jnp.dot(
+            weights.astype(jnp.bfloat16), kv[slot, head, 1], preferred_element_type=jnp.float32
+        )
+        return product, functools.reduce(jnp.add, lane_parts(weights))
+
+    def step(head, slots, valid, first=False):
+        @pl.loop(0, group // query_heads)
         def _(index):
-            sub = index // tiles
-            start = pl.multiple_of(lax.rem(index, tiles) * query_tile, query_tile)
             state = pl.ds(pl.multiple_of(index * query_tile, query_tile), query_tile)
-            q = q_buf[head * group + sub, pl.ds(start, query_tile), :]
+            q = q_buf[head, state, :]
             scores = []
-            for slot in slots:
+            top = None
+            for slot, good in zip(slots, valid):
                 part = scores_of(q, slot, head)
                 if slot == OWN:
-                    row = start + lax.broadcasted_iota(jnp.int32, part.shape, 0)
-                    column = lax.broadcasted_iota(jnp.int32, part.shape, 1)
-                    near = column <= row
+                    square = (rows, part.shape[1])
+                    row = lax.broadcasted_iota(jnp.int32, square, 0)
+                    near = lax.broadcasted_iota(jnp.int32, square, 1) <= row
+                    near = jnp.concatenate([near] * query_heads, 0) if query_heads > 1 else near
                     far = scores_of(q, FAR, head)
-                    far = jnp.where(plane >= 2, far, negative_fill)
+                    far = jnp.where(far_ok, far, negative_fill)
                     part = jnp.where(near, part, far)
                 scores.append(part)
-            top = functools.reduce(jnp.maximum, scores)
+                peaks = functools.reduce(jnp.maximum, lane_parts(part))
+                if good is not None:
+                    peaks = jnp.where(good, peaks, negative_fill)
+                top = peaks if top is None else jnp.maximum(top, peaks)
             top = jnp.max(top, axis=1, keepdims=True)
             if not first:
                 before = peak[state, :]
@@ -135,46 +146,29 @@
             else:
                 peak[state, :] = jnp.broadcast_to(top, (query_tile, HEAD_DIM))
             top = top[:, :1]
-            total = None
-            for slot, part in zip(slots, scores):
-                weights = jnp.exp2((part - top) * factor)
+            pieces = []
+            for slot, part, good in zip(slots, scores, valid):
+                base = top if good is None else jnp.where(good, top, -negative_fill)
+                weights = jnp.exp2((part - base) * factor)
                 if slot == OWN:
-                    product = product_of(jnp.where(near, weights, 0.0), OWN, head)
-                    product += product_of(jnp.where(near, 0.0, weights), FAR, head)
+                    pieces.append(product_of(jnp.where(near, weights, 0.0), OWN, head))
+                    pieces.append(product_of(jnp.where(near, 0.0, weights), FAR, head))
                 else:
-                    product = product_of(weights, slot, head)
-                total = product if total is None else total + product
-            if first:
-                acc[state, :] = total
-            else:
-                acc[state, :HEAD_DIM] = acc[state, :HEAD_DIM] * fade + total[:, :HEAD_DIM]
-                acc[state, HEAD_DIM:] = acc[state, HEAD_DIM:] * fade + total[:, HEAD_DIM:]
-
-    def steps(head, valid, all_valid, slots, first=False):
-        @pl.when(all_valid)
-        def _():
-            step(head, slots, first)
-
-        @pl.when(jnp.logical_not(all_valid))
-        def _():
-            for at, (slot, good) in enumerate(zip(slots, valid)):
-                if good is None:
-                    step(head, (slot,), first and at == 0)
-                else:
-                    pl.when(good)(functools.partial(step, head, (slot,)))
+                    pieces.append(product_of(weights, slot, head))
+            product, lanes = (functools.reduce(jnp.add, each) for each in zip(*pieces))
+            if not first:
+                product += acc[state, :HEAD_DIM] * fade
+                lanes += acc[state, HEAD_DIM:] * fade
+            acc[state, :HEAD_DIM] = product
+            acc[state, HEAD_DIM:] = lanes
 
     def finish(head):
         for sub in range(group):
             spot = pl.ds(sub * rows, rows)
             o_buf[head * group + sub] = (
-                acc[spot, :HEAD_DIM] / acc[spot, HEAD_DIM:]
+                acc[spot, :HEAD_DIM] / jnp.sum(acc[spot, HEAD_DIM:], axis=1, keepdims=True)
             ).astype(o_buf.dtype)
             out_copy(head, sub).start()
-
-    near_ok = plane >= 1
-    far_ok = plane >= 2
-    mix_a_ok = (plane >= 2) | (bit_a == 1)
-    mix_b_ok = (plane >= 2) | (bit_b == 1)
 
     @pl.loop(0, local + 1)
     def _(now):
@@ -192,7 +186,7 @@
             transfer(last, MIX_A).wait_recv()
             transfer(last, MIX_C).start()
             transfer(last, NEAR_C).start()
-            steps(last, (near_ok, mix_a_ok, mix_b_ok), far_ok, (NEAR_B, MIX_A, MIX_B))
+            step(last, (NEAR_B, MIX_A, MIX_B), (near_ok, mix_a_ok, mix_b_ok))
 
         @pl.when(now < local)
         def _():
@@ -205,7 +199,7 @@
         def _():
             transfer(last, MIX_C).wait_recv()
             transfer(last, NEAR_C).wait_recv()
-            steps(last, (near_ok, mix_b_ok), far_ok, (NEAR_C, MIX_C))
+            step(last, (NEAR_C, MIX_C), (near_ok, mix_b_ok))
             finish(last)
 
         @pl.when(now < local)
@@ -217,7 +211,7 @@
             transfer(now, NEAR_B).wait_recv()
             for sub in range(group):
                 q_copy(now, sub).wait()
-            steps(now, (None, near_ok, near_ok), near_ok, (OWN, NEAR, NEAR_A), True)
+            step(now, (OWN, NEAR, NEAR_A), (None, near_ok, near_ok), True)
 
     @pl.loop(0, local)
     def _(head):
@@ -244,7 +238,7 @@
         in_specs=[hbm] * 3,
         out_specs=hbm,
         scratch_shapes=[
-            pltpu.VMEM((heads, rows, HEAD_DIM), jnp.bfloat16),
+            pltpu.VMEM((local, group * rows, HEAD_DIM), jnp.bfloat16),
             pltpu.VMEM((heads, rows, HEAD_DIM), jnp.bfloat16),
             pltpu.VMEM((9, local, 2, rows, HEAD_DIM), jnp.bfloat16),
             pltpu.VMEM((group * rows, 2 * HEAD_DIM), jnp.float32),

time: 188 us -> 121 us (0.64)
  the two profiles are of different devices: /device:TPU:14 before, /device:TPU:0 now
where the time goes in v2:
time: 121 us
  Pallas kernels  111 us (92%)
  other arithmetic  5.88 us (5%)
  local copies, waits for them, and re-layouts  3.17 us (3%)
    pallas_call x1, Pallas kernels, attend(): pl.pallas_call(kernel, out_shape=jax.ShapeDtypeStruct(queries.shape, jnp....  111 us
    unnamed x5, local copies, waits for them, and re-layouts  3.17 us
  transfers between devices with their start and end apart: 1, of which 0 were waited for; matrix products, arithmetic and copies ran while one was open for 2% of the time, Pallas kernels for 91%

profile of v2, /device:TPU:0, one launch (start us, length us, event | category | flops | bytes accessed | tf_op | source)
XLA Modules:
  0.0 120.9 jit_solution(10189793822367731858)
XLA Ops:
  0.6 1.2 convert_reduce_fusion
  1.8 1.2 reduce_max.26
  3.1 0.6 collective-permute-start
  3.6 1.1 convert_reduce_fusion.1
  4.7 0.0 copy-start
  4.8 1.1 bitcast_reduce_fusion
  5.9 110.6 %shard_map.74 = bf16[512,2048]{1,0:T(8,128)(2,1)} custom-call(bf16[512,2048]{1,0:T(8,128)(2,1)} %q_hbm.1, bf16[512,512]{1,0:T(8,128)(2,1)} %k_hbm.1, bf16[512,512]{1,0:T(8,128)(2,1)} %v_hbm.1), custom_call_target="tpu_custom_call" | custom-call | flops 17179869184 | bytes 4194304 | tf_op jit(solution)/shard_map/pallas_call | solution.py:235
  116.5 0.0 copy-done
  116.5 0.6 fusion
  117.1 0.0 collective-permute-done
  117.2 0.0 copy-start.1
  117.2 0.6 subtract_multiply_fusion
  117.8 3.2 %copy.9 = bf16[512,2048]{1,0:T(8,128)(2,1)} copy(bf16[512,2048]{1,0:T(8,128)(2,1)} %shard_map.74) | data formatting | bytes 4194304
  120.9 0.0 copy-done.1
  (5 shorter events, 0.0 us)
Async XLA Ops:
  3.1 114.1 %collective-permute-start = (f32[2,512]{1,0:T(2,128)S(1)}, f32[2,512]{1,0:T(2,128)S(1)}, u32[]{:S(2)}, u32[]{:S(2)}) collective-permute-start(f32[2,512]{1,0:T(2,128)S(1)} %pad_maximum_fusion), channel_id=1, source_target_pairs={{0,1},{1,0},{2,3},{3,2},{4,5},{5,4},{6,7},{7,6},{8,9},{9,8},{10,11... | collective-permute-start | bytes 12296 | tf_op jit(solution)/shard_map/ppermute | solution.py:267
  4.7 111.8 %copy-start = (f32[4,512]{1,0:T(4,128)}, f32[4,512]{1,0:T(4,128)S(1)}, u32[]{:S(2)}) copy-start(f32[4,512]{1,0:T(4,128)S(1)} %convert_reduce_fusion.1) | copy-start | bytes 24580
  117.2 3.8 %copy-start.1 = (f32[1,512]{1,0:T(1,128)}, f32[1,512]{1,0:T(1,128)S(1)}, u32[]{:S(2)}) copy-start(f32[1,512]{1,0:T(1,128)S(1)} %get-tuple-element.6) | copy-start | bytes 6148
